TPU v7x, 32 devices: a whole 2x2x4 slice. The times are simulated.
32 devices in a mesh: section: 1, srv: 16 (over z, x, core), tp: 2 (over y).
Axes of the slice: x: 2, y: 2, z: 4, core: 2. Of those that a mesh axis runs over, the one named last changes fastest.
Arguments:
- queries: bfloat16 [2048, 4096], P(('section', 'srv'), 'tp'), may hold values from -40 to 40
- keys: bfloat16 [2048, 512], P(('section', 'srv'), 'tp'), may hold values from -40 to 40
- values: bfloat16 [2048, 512], P(('section', 'srv'), 'tp'), may hold values from -6 to 6
- residual: bfloat16 [2048, 4096], P(('section', 'srv'), 'tp'), may hold values from -6 to 6
- out_weight: bfloat16 [4096, 4096], P('tp', ('section', 'srv')), may hold values from -0.1875 to 0.1875
- norm_gain: float32 [4096], P('tp'), may hold values from 0.25 to 1.75
- level_shift: float32 [8, 4096], P(None, 'tp'), may hold values from -3 to 3
- doc_lengths: int32 [1, 4], P('section'), may hold values from 1 to 64, 128 in all within a row
- noise_level: int32 [1, 4], P('section'), may hold values from 0 to 7
Outputs:
- normed: bfloat16 [2048, 4096], P(('section', 'srv'), 'tp')
Inputs may be any that keep to these rules, and one draw needn't show every extreme that they name: `doc_lengths`: each micro-batch's lengths sum to 128.
All inputs are finite; a program needn't handle non-finite values.
Results may differ from a plain program's by a relative error of at most 0.013.
Values may be sent and summed in bfloat16 or wider, within the bound.
No kernel may reach another device: no remote copies, remote signals or barrier semaphores. Data moves between devices by JAX's collectives and lax.ppermute only.
A program may use at most 64 MiB of HBM per device.

v0:
```python
import functools
import jax
import jax.numpy as jnp
from jax import lax
from jax.experimental import pallas as pl
from jax.experimental.pallas import tpu as pltpu
from jax.sharding import PartitionSpec as P


HEAD_SIZE = 128
BLK = 16
LOW_BITS = 2
FIRST_STRETCHES = 2


def flipped(block, mask, axis="srv"):
    devices = range(lax.axis_size(axis))
    return lax.ppermute(block, axis, [(i, i ^ mask) for i in devices])


def shifted(block, axis, distance):
    devices = range(lax.axis_size(axis))
    route = [(i - distance, i) for i in devices if i - distance in devices]
    return lax.ppermute(block, axis, route)


def attention_kernel(kv_heads, groups, info, q_ref, a_ref, b_ref, o_ref, q_s, s_s, m_s, l_s, acc_s):
    rows = q_ref.shape[0]
    pairs = a_ref.shape[0]
    docs = info.shape[0] - 1 - 2 * pairs
    scale = HEAD_SIZE ** (-0.5)
    base = info[0]
    position = base + lax.broadcasted_iota(jnp.int32, (rows, 2 * rows), 0)
    first = jnp.zeros((rows, 2 * rows), jnp.int32)
    lowest = jnp.int32(0)
    begin = jnp.int32(0)
    for d in range(docs):
        end = begin + info[1 + 2 * pairs + d] * BLK
        first = jnp.where((position >= begin) & (position < end), begin, first)
        lowest = jnp.where((base >= begin) & (base < end), begin, lowest)
        begin = end
    limit = (position // BLK + 1) * BLK
    lane = lax.broadcasted_iota(jnp.int32, (rows, 2 * rows), 1)

    def active(p):
        low = jnp.minimum(info[1 + 2 * p], info[2 + 2 * p])
        return (low + 2 * rows > lowest) & (low < base + rows)

    for h in range(kv_heads):
        for g in range(groups):
            at = (h * groups + g) * HEAD_SIZE
            q_s[g * rows : (g + 1) * rows, :] = q_ref[:, at : at + HEAD_SIZE]
        m_s[...] = jnp.full(m_s.shape, -1e30, jnp.float32)
        l_s[...] = jnp.zeros(l_s.shape, jnp.float32)
        acc_s[...] = jnp.zeros(acc_s.shape, jnp.float32)
        k_at = h * HEAD_SIZE
        v_at = (kv_heads + h) * HEAD_SIZE

        def score(p, carry):
            @pl.when(active(p))
            def _():
                k = jnp.concatenate(
                    [a_ref[p, :, k_at : k_at + HEAD_SIZE], b_ref[p, :, k_at : k_at + HEAD_SIZE]], 0
                )
                key_pos = jnp.where(lane < rows, info[1 + 2 * p] + lane, info[2 + 2 * p] + lane - rows)
                mask = (key_pos >= first) & (key_pos < limit)
                for g in range(groups):
                    span = slice(g * rows, (g + 1) * rows)
                    s = lax.dot_general(
                        q_s[span, :], k, (((1,), (1,)), ((), ())), preferred_element_type=jnp.float32
                    )
                    s = jnp.where(mask, s * scale, -1e30)
                    s_s[p, span, :] = s
                    m_s[span, :] = jnp.maximum(m_s[span, :], jnp.maximum(s[:, :rows], s[:, rows:]))

            return carry

        lax.fori_loop(0, pairs, score, 0)
        for g in range(groups):
            span = slice(g * rows, (g + 1) * rows)
            m_s[span, :] = jnp.broadcast_to(jnp.max(m_s[span, :], axis=1, keepdims=True), (rows, rows))

        def weigh(p, carry):
            @pl.when(active(p))
            def _():
                v = jnp.concatenate(
                    [a_ref[p, :, v_at : v_at + HEAD_SIZE], b_ref[p, :, v_at : v_at + HEAD_SIZE]], 0
                )
                for g in range(groups):
                    span = slice(g * rows, (g + 1) * rows)
                    m = m_s[span, :]
                    w = jnp.exp(s_s[p, span, :] - jnp.concatenate([m, m], 1))
                    l_s[span, :] += w[:, :rows] + w[:, rows:]
                    acc_s[span, :] += jnp.dot(
                        w.astype(jnp.bfloat16), v, preferred_element_type=jnp.float32
                    )

            return carry

        lax.fori_loop(0, pairs, weigh, 0)
        for g in range(groups):
            span = slice(g * rows, (g + 1) * rows)
            at = (h * groups + g) * HEAD_SIZE
            total = jnp.sum(l_s[span, :], axis=1, keepdims=True)
            o_ref[:, at : at + HEAD_SIZE] = (acc_s[span, :] / total).astype(o_ref.dtype)


def attend(info, queries, near, far):
    rows, width = queries.shape
    kv_heads = near.shape[2] // (2 * HEAD_SIZE)
    groups = width // HEAD_SIZE // kv_heads
    pairs = near.shape[0]
    tall = groups * rows
    vmem = pl.BlockSpec(memory_space=pltpu.VMEM)
    return pl.pallas_call(
        functools.partial(attention_kernel, kv_heads, groups),
        out_shape=jax.ShapeDtypeStruct((rows, width), jnp.bfloat16),
        in_specs=[pl.BlockSpec(memory_space=pltpu.SMEM), vmem, vmem, vmem],
        out_specs=vmem,
        scratch_shapes=[
            pltpu.VMEM((tall, HEAD_SIZE), jnp.bfloat16),
            pltpu.VMEM((pairs, tall, 2 * rows), jnp.float32),
            pltpu.VMEM((tall, rows), jnp.float32),
            pltpu.VMEM((tall, rows), jnp.float32),
            pltpu.VMEM((tall, HEAD_SIZE), jnp.float32),
        ],
        cost_estimate=pl.CostEstimate(
            flops=8 * rows * width * pairs * rows,
            bytes_accessed=4 * rows * width,
            transcendentals=2 * rows * rows * pairs * width // HEAD_SIZE,
        ),
        compiler_params=pltpu.CompilerParams(vmem_limit_bytes=40 * 1024 * 1024),
        name="attend",
    )(info, queries, near, far)


def ordered(parts, bit):
    low = jnp.concatenate(parts, axis=-1)
    high = jnp.concatenate(parts[::-1], axis=-1)
    return jnp.where(bit == 0, low, high)


def project_kernel(count, layout, cut, *refs):
    rows = refs[:count]
    arrays = refs[count:-1]
    out = refs[-1]
    columns = []
    for segments in layout:
        taken = [arrays[n][:, at : at + cut] for n, at in segments]
        columns.append(taken[0] if len(taken) == 1 else jnp.concatenate(taken, axis=0))
    w = columns[0] if len(columns) == 1 else jnp.concatenate(columns, axis=1)
    size = rows[0].shape[0]
    for i in range(count):
        out[i * size : (i + 1) * size, :] = jnp.dot(
            rows[i][...], w, preferred_element_type=jnp.float32
        ).astype(out.dtype)


def project(rows, parts, cut):
    height = sum(r.shape[0] for r in rows)
    depth = rows[0].shape[1]
    width = cut * len(parts)
    if cut % 128:
        columns = [
            jnp.concatenate([w[:, at : at + cut] for w, at in segments], 0) for segments in parts
        ]
        joined = jnp.dot(
            jnp.concatenate(rows, 0), jnp.concatenate(columns, 1), preferred_element_type=jnp.float32
        )
        return joined.astype(jnp.bfloat16)
    arrays = [w for segments in parts for w, _ in segments]
    layout, n = [], 0
    for segments in parts:
        layout.append(tuple((n + i, at) for i, (_, at) in enumerate(segments)))
        n += len(segments)
    vmem = pl.BlockSpec(memory_space=pltpu.VMEM)
    return pl.pallas_call(
        functools.partial(project_kernel, len(rows), tuple(layout), cut),
        out_shape=jax.ShapeDtypeStruct((height, width), jnp.bfloat16),
        in_specs=[vmem] * (len(rows) + len(arrays)),
        out_specs=vmem,
        cost_estimate=pl.CostEstimate(
            flops=2 * height * width * depth,
            bytes_accessed=2 * depth * (height + width),
            transcendentals=0,
        ),
        compiler_params=pltpu.CompilerParams(vmem_limit_bytes=24 * 1024 * 1024),
        name="project",
    )(*rows, *arrays)


def on_device(
    queries, keys, values, residual, out_weight, norm_gain, level_shift, doc_lengths, noise_level
):
    rows = queries.shape[0]
    here = lax.axis_index("srv")
    devices = lax.axis_size("srv")
    sections = lax.axis_size("section")
    peers = lax.axis_size("tp")
    mine = lax.axis_index("tp")
    whole_index = lax.axis_index("section") * devices + here
    bits = devices.bit_length() - 1
    low = 1 << LOW_BITS
    width = out_weight.shape[1]
    chunks = max(1, width // 128)
    cut = width // chunks

    kv = jnp.concatenate([keys, values], axis=1)
    turns = -(-(devices // 2) // low)
    back = []
    for k in range(1, turns + 1):
        back.append(shifted(kv, "srv", low * k))
    beside = flipped(kv, 2)
    beside_back = flipped(jnp.stack(back), 2)
    near = jnp.concatenate([jnp.stack([kv] + back + [beside]), beside_back], axis=0)
    far = flipped(near, 1)
    own = here % low
    block = here - own
    order = [(k, 0) for k in range(turns + 1)] + [(k, 2) for k in range(turns + 1)]
    spots = []
    for k, x in order:
        for c in (0, 1):
            spots.append((block - low * k + (own ^ (x + c))) * rows)
    info = jnp.stack([here * rows] + spots).astype(jnp.int32)
    info = jnp.concatenate([info, doc_lengths[0].astype(jnp.int32)])

    depth = out_weight.shape[0]
    pieces_of = []
    for j in range(chunks):
        stretches = FIRST_STRETCHES if j == 0 else 1
        pieces_of.append([(j, n, depth // stretches) for n in range(stretches)])
    held = []
    for j in range(chunks):
        segments = []
        for _, n, size in pieces_of[j]:
            got = {0: out_weight[n * size : (n + 1) * size, j * cut : (j + 1) * cut]}
            for b in range(3, bits):
                got.update({r | (1 << b): flipped(w, 1 << b) for r, w in list(got.items())})
            hop = 1
            while hop < sections:
                got.update(
                    {r | (hop * devices): flipped(w, hop, "section") for r, w in list(got.items())}
                )
                hop *= 2
            segments.append(got)
        held.append(segments)
    beside_own = flipped(out_weight, 1)
    sources = []
    for j in range(chunks):
        found = {0: [(out_weight, j * cut)], 1: [(beside_own, j * cut)]}
        for got in held[j]:
            for r, w in got.items():
                if r:
                    found.setdefault(r, []).append((w, 0))
                    found.setdefault(r | 1, []).append((flipped(w, 1), 0))
        sources.append(found)

    attended = attend(info, queries, near, far)
    row_keys = (0, 2, 4, 6)
    across = flipped(attended, 4)
    gathered = [attended, flipped(attended, 2), across]
    gathered.append(flipped(across, 2))

    lengths = doc_lengths[0] * BLK
    ends = jnp.cumsum(lengths)
    starts = ends - lengths
    positions = here * rows + jnp.arange(rows, dtype=jnp.int32)
    member = (positions[:, None] >= starts[None, :]) & (positions[:, None] < ends[None, :])
    level = jnp.sum(jnp.where(member, noise_level[0][None, :], 0), axis=1)
    onehot = (level[:, None] == jnp.arange(level_shift.shape[0], dtype=jnp.int32)[None, :]).astype(
        jnp.float32
    )
    shift = jnp.dot(onehot, level_shift, precision=lax.Precision.HIGHEST)
    factor = norm_gain[None, :] * (1.0 + shift)
    base, factor, gathered[1] = lax.optimization_barrier(
        (residual.astype(jnp.float32), factor, gathered[1])
    )

    span = sections * devices // peers
    turn = whole_index // span ^ mine
    lower = sorted(r for r in sources[0] if r < span)
    pieces = {}
    for j in range(chunks):
        by_part = [
            project(gathered, [sources[j][part * span + r] for r in lower], cut)
            for part in range(peers)
        ]

        def chosen(e):
            value = by_part[0]
            for part in range(1, peers):
                value = jnp.where((turn ^ e) == part, by_part[part], value)
            return value

        total = chosen(0).astype(jnp.float32)
        for e in range(1, peers):
            total = total + flipped(chosen(e), e, "tp").astype(jnp.float32)
        for i, r in enumerate(row_keys):
            piece = total[i * rows : (i + 1) * rows]
            if r:
                piece = flipped(piece.astype(jnp.bfloat16), r).astype(jnp.float32)
            for n, a in enumerate(lower):
                pieces.setdefault(a ^ r, []).append(piece[:, n * cut : (n + 1) * cut])
    pieces = {r: jnp.concatenate(p, axis=1) for r, p in pieces.items()}
    b = 1
    while len(pieces) > 1:
        pieces = {
            r: ordered([pieces[r], pieces[r | b]], (whole_index // b) % 2)
            for r in pieces
            if not r & b
        }
        b *= 2
    hidden = pieces[0] + base

    squares = jnp.sum(hidden * hidden, axis=1)
    hop = 1
    while hop < peers:
        squares = squares + flipped(squares, hop, "tp")
        hop *= 2
    inverse = lax.rsqrt(squares / (hidden.shape[1] * peers) + 1e-06)[:, None]
    normed = hidden * inverse * factor
    return normed.astype(jnp.bfloat16)


def solution(mesh):
    placed = (
        P(("section", "srv"), "tp"),
        P(("section", "srv"), "tp"),
        P(("section", "srv"), "tp"),
        P(("section", "srv"), "tp"),
        P("tp", ("section", "srv")),
        P("tp"),
        P(None, "tp"),
        P("section", None),
        P("section", None),
    )
    return jax.shard_map(
        on_device,
        mesh=mesh,
        in_specs=placed,
        out_specs=P(("section", "srv"), "tp"),
        check_vma=False,
    )
```

profile of v0, /device:TPU:0, one launch (start us, length us, event | category | flops | bytes accessed | tf_op | source)
XLA Modules:
  0.0 109.7 jit_solution(4376825338031246348)
XLA Ops:
  0.9 3.0 %collective-permute-start.2 = (bf16[128,512]{1,0:T(8,128)(2,1)S(1)}, bf16[128,512]{1,0:T(8,128)(2,1)S(1)}, u32[]{:S(2)}, u32[]{:S(2)}) collective-permute-start(bf16[128,512]{1,0:T(8,128)(2,1)S(1)} %constant_dynamic-update-slice_fusion), channel_id=1, source_target_pairs={{0,4},{2,6},{4,0},{6,2},{8,12},{10,14},{12,8},{14,10},{16,20},{18,... | collective-permute-start | bytes 393224 | tf_op jit(solution)/shard_map/ppermute | solution.py:18
  3.9 4.5 %collective-permute-start.1 = (bf16[128,512]{1,0:T(8,128)(2,1)S(1)}, bf16[128,512]{1,0:T(8,128)(2,1)S(1)}, u32[]{:S(2)}, u32[]{:S(2)}) collective-permute-start(bf16[128,512]{1,0:T(8,128)(2,1)S(1)} %constant_dynamic-update-slice_fusion), channel_id=1, source_target_pairs={{0,16},{2,18},{4,20},{6,22},{8,24},{10,26},{12,28},{14,30},{1,17},... | collective-permute-start | bytes 393224 | tf_op jit(solution)/shard_map/ppermute | solution.py:24
  8.4 3.5 %collective-permute-start = (bf16[128,512]{1,0:T(8,128)(2,1)S(1)}, bf16[128,512]{1,0:T(8,128)(2,1)S(1)}, u32[]{:S(2)}, u32[]{:S(2)}) collective-permute-start(bf16[128,512]{1,0:T(8,128)(2,1)S(1)} %constant_dynamic-update-slice_fusion), channel_id=1, source_target_pairs={{0,8},{2,10},{4,12},{6,14},{8,16},{10,18},{12,20},{14,22},{16,24},... | collective-permute-start | bytes 393224 | tf_op jit(solution)/shard_map/ppermute | solution.py:24
  12.0 2.5 %collective-permute-done = bf16[128,512]{1,0:T(8,128)(2,1)S(1)} collective-permute-done((bf16[128,512]{1,0:T(8,128)(2,1)S(1)}, bf16[128,512]{1,0:T(8,128)(2,1)S(1)}, u32[]{:S(2)}, u32[]{:S(2)}) %collective-permute-start) | collective-permute-done | bytes 131104 | tf_op jit(solution)/shard_map/ppermute | solution.py:24
  15.1 6.0 %collective-permute-done.3 = bf16[2,128,512]{2,1,0:T(8,128)(2,1)S(1)} collective-permute-done((bf16[2,128,512]{2,1,0:T(8,128)(2,1)S(1)}, bf16[2,128,512]{2,1,0:T(8,128)(2,1)S(1)}, u32[]{:S(2)}, u32[]{:S(2)}) %collective-permute-start.3) | collective-permute-done | bytes 262176 | tf_op jit(solution)/shard_map/ppermute | solution.py:18
  22.1 7.1 %collective-permute-start.14 = (bf16[2048,128]{1,0:T(8,128)(2,1)}, bf16[2048,128]{1,0:T(8,128)(2,1)}, u32[]{:S(2)}, u32[]{:S(2)}) collective-permute-start(bf16[2048,128]{1,0:T(8,128)(2,1)} %slice.90), channel_id=1, source_target_pairs={{0,16},{2,18},{4,20},{6,22},{8,24},{10,26},{12,28},{14,30},{16,0},... | collective-permute-start | bytes 1572872 | tf_op jit(solution)/shard_map/ppermute | solution.py:18
  31.0 3.3 %attend.1.refs_0_ = bf16[128,2048]{1,0:T(8,128)(2,1)S(1)} custom-call(s32[17]{0:T(128)S(1)} %concatenate.67.info, bf16[128,2048]{1,0:T(8,128)(2,1)S(1)} %copy-done.2, bf16[6,128,512]{2,1,0:T(8,128)(2,1)S(1)} %constant_dynamic-update-slice_fusion.2.a_ref, bf16[6,128,512]{2,1,0:T(8,128)(2,1)S(1)} %collective-permute-done.4.b_ref), custom_call_target="tpu_custom_call" | custom-call | flops 1610612736 | bytes 1048576 | tf_op jit(solution)/shard_map/attend/pallas_call | solution.py:115
  36.4 2.2 %collective-permute-start.9 = (bf16[1024,128]{1,0:T(8,128)(2,1)}, bf16[1024,128]{1,0:T(8,128)(2,1)S(1)}, u32[]{:S(2)}, u32[]{:S(2)}) collective-permute-start(bf16[1024,128]{1,0:T(8,128)(2,1)} %get-tuple-element.15), channel_id=1, source_target_pairs={{0,16},{2,18},{4,20},{6,22},{8,24},{10,26},{12,28},{14,30},{16,0},... | collective-permute-start | bytes 786440 | tf_op jit(solution)/shard_map/ppermute | solution.py:18
  38.9 15.2 %collective-permute-done.14.refs_4_ = bf16[2048,128]{1,0:T(8,128)(2,1)} collective-permute-done((bf16[2048,128]{1,0:T(8,128)(2,1)}, bf16[2048,128]{1,0:T(8,128)(2,1)}, u32[]{:S(2)}, u32[]{:S(2)}) %collective-permute-start.14) | collective-permute-done | bytes 524320 | tf_op jit(solution)/shard_map/ppermute | solution.py:18
  54.6 10.4 %collective-permute-done.6.refs_2_ = bf16[128,2048]{1,0:T(8,128)(2,1)S(1)} collective-permute-done((bf16[128,2048]{1,0:T(8,128)(2,1)S(1)}, bf16[128,2048]{1,0:T(8,128)(2,1)S(1)}, u32[]{:S(2)}, u32[]{:S(2)}) %collective-permute-start.6) | collective-permute-done | bytes 524320 | tf_op jit(solution)/shard_map/ppermute | solution.py:18
  65.0 1.8 %collective-permute-start.7 = (bf16[128,2048]{1,0:T(8,128)(2,1)S(1)}, bf16[128,2048]{1,0:T(8,128)(2,1)S(1)}, u32[]{:S(2)}, u32[]{:S(2)}) collective-permute-start(bf16[128,2048]{1,0:T(8,128)(2,1)S(1)} %collective-permute-done.6.refs_2_), channel_id=1, source_target_pairs={{0,4},{2,6},{4,0},{6,2},{8,12},{10,14},{12,8},{14,10},{16,20},{18,... | collective-permute-start | bytes 1572872 | tf_op jit(solution)/shard_map/ppermute | solution.py:18
  69.4 10.5 %collective-permute-done.8.refs_4_ = bf16[1024,128]{1,0:T(8,128)(2,1)} collective-permute-done((bf16[1024,128]{1,0:T(8,128)(2,1)}, bf16[1024,128]{1,0:T(8,128)(2,1)}, u32[]{:S(2)}, u32[]{:S(2)}) %collective-permute-start.8) | collective-permute-done | bytes 262176 | tf_op jit(solution)/shard_map/ppermute | solution.py:18
  80.4 1.9 %project.6 = bf16[512,256]{1,0:T(8,128)(2,1)S(1)} custom-call(bf16[128,2048]{1,0:T(8,128)(2,1)S(1)} %attend.1.refs_0_, bf16[128,2048]{1,0:T(8,128)(2,1)S(1)} %collective-permute-done.5.refs_1_, bf16[128,2048]{1,0:T(8,128)(2,1)S(1)} %collective-permute-done.6.refs_2_, bf16[128,2048]{1,0:T(8,128)(2,1)S(1)} %collective-permute-done.7.refs_3_, ...), custom_call_target="tpu_custom_call" | custom-call | flops 536870912 | bytes 3145728 | tf_op jit(solution)/shard_map/project/pallas_call | solution.py:177
  82.3 1.9 %project.7 = bf16[512,256]{1,0:T(8,128)(2,1)S(1)} custom-call(bf16[128,2048]{1,0:T(8,128)(2,1)S(1)} %attend.1.refs_0_, bf16[128,2048]{1,0:T(8,128)(2,1)S(1)} %collective-permute-done.5.refs_1_, bf16[128,2048]{1,0:T(8,128)(2,1)S(1)} %collective-permute-done.6.refs_2_, bf16[128,2048]{1,0:T(8,128)(2,1)S(1)} %collective-permute-done.7.refs_3_, ...), custom_call_target="tpu_custom_call" | custom-call | flops 536870912 | bytes 3145728 | tf_op jit(solution)/shard_map/project/pallas_call | solution.py:177
  84.3 1.6 %collective-permute-start.16 = (bf16[512,256]{1,0:T(8,128)(2,1)S(1)}, bf16[512,256]{1,0:T(8,128)(2,1)S(1)}, u32[]{:S(2)}, u32[]{:S(2)}) collective-permute-start(bf16[512,256]{1,0:T(8,128)(2,1)S(1)} %broadcast_select_fusion), channel_id=1, source_target_pairs={{0,1},{1,0},{2,3},{3,2},{4,5},{5,4},{6,7},{7,6},{8,9},{9,8},{10,11... | collective-permute-start | bytes 786440 | tf_op jit(solution)/shard_map/ppermute | solution.py:18
  85.9 1.9 %project.5 = bf16[512,256]{1,0:T(8,128)(2,1)S(1)} custom-call(bf16[128,2048]{1,0:T(8,128)(2,1)S(1)} %attend.1.refs_0_, bf16[128,2048]{1,0:T(8,128)(2,1)S(1)} %collective-permute-done.5.refs_1_, bf16[128,2048]{1,0:T(8,128)(2,1)S(1)} %collective-permute-done.6.refs_2_, bf16[128,2048]{1,0:T(8,128)(2,1)S(1)} %collective-permute-done.7.refs_3_, ...), custom_call_target="tpu_custom_call" | custom-call | flops 536870912 | bytes 3145728 | tf_op jit(solution)/shard_map/project/pallas_call | solution.py:177
  87.9 1.7 %project.4 = bf16[512,256]{1,0:T(8,128)(2,1)S(1)} custom-call(bf16[128,2048]{1,0:T(8,128)(2,1)S(1)} %attend.1.refs_0_, bf16[128,2048]{1,0:T(8,128)(2,1)S(1)} %collective-permute-done.5.refs_1_, bf16[128,2048]{1,0:T(8,128)(2,1)S(1)} %collective-permute-done.6.refs_2_, bf16[128,2048]{1,0:T(8,128)(2,1)S(1)} %collective-permute-done.7.refs_3_, ...), custom_call_target="tpu_custom_call" | custom-call | flops 536870912 | bytes 3145728 | tf_op jit(solution)/shard_map/project/pallas_call | solution.py:177
  90.2 3.1 %collective-permute-done.16 = bf16[512,256]{1,0:T(8,128)(2,1)S(1)} collective-permute-done((bf16[512,256]{1,0:T(8,128)(2,1)S(1)}, bf16[512,256]{1,0:T(8,128)(2,1)S(1)}, u32[]{:S(2)}, u32[]{:S(2)}) %collective-permute-start.16) | collective-permute-done | bytes 262176 | tf_op jit(solution)/shard_map/ppermute | solution.py:18
  93.5 1.7 %collective-permute-start.22 = (bf16[128,256]{1,0:T(8,128)(2,1)S(1)}, bf16[128,256]{1,0:T(8,128)(2,1)S(1)}, u32[]{:S(2)}, u32[]{:S(2)}) collective-permute-start(bf16[128,256]{1,0:T(8,128)(2,1)S(1)} %get-tuple-element.25), channel_id=1, source_target_pairs={{0,12},{2,14},{4,8},{6,10},{8,4},{10,6},{12,0},{14,2},{16,28},{18,... | collective-permute-start | bytes 196616 | tf_op jit(solution)/shard_map/ppermute | solution.py:18
  95.2 1.7 %collective-permute-start.18 = (bf16[128,256]{1,0:T(8,128)(2,1)S(1)}, bf16[128,256]{1,0:T(8,128)(2,1)S(1)}, u32[]{:S(2)}, u32[]{:S(2)}) collective-permute-start(bf16[128,256]{1,0:T(8,128)(2,1)S(1)} %get-tuple-element.26), channel_id=1, source_target_pairs={{0,4},{2,6},{4,0},{6,2},{8,12},{10,14},{12,8},{14,10},{16,20},{18,... | collective-permute-start | bytes 196616 | tf_op jit(solution)/shard_map/ppermute | solution.py:18
  98.4 1.7 %collective-permute-start.21 = (bf16[128,256]{1,0:T(8,128)(2,1)S(1)}, bf16[128,256]{1,0:T(8,128)(2,1)S(1)}, u32[]{:S(2)}, u32[]{:S(2)}) collective-permute-start(bf16[128,256]{1,0:T(8,128)(2,1)S(1)} %get-tuple-element.22), channel_id=1, source_target_pairs={{0,12},{2,14},{4,8},{6,10},{8,4},{10,6},{12,0},{14,2},{16,28},{18,... | collective-permute-start | bytes 196616 | tf_op jit(solution)/shard_map/ppermute | solution.py:18
  100.2 1.8 %collective-permute-start.17 = (bf16[128,256]{1,0:T(8,128)(2,1)S(1)}, bf16[128,256]{1,0:T(8,128)(2,1)S(1)}, u32[]{:S(2)}, u32[]{:S(2)}) collective-permute-start(bf16[128,256]{1,0:T(8,128)(2,1)S(1)} %get-tuple-element.23), channel_id=1, source_target_pairs={{0,4},{2,6},{4,0},{6,2},{8,12},{10,14},{12,8},{14,10},{16,20},{18,... | collective-permute-start | bytes 196616 | tf_op jit(solution)/shard_map/ppermute | solution.py:18
  104.9 1.6 %collective-permute-start.23 = (f32[128]{0:T(128)S(1)}, f32[128]{0:T(128)S(1)}, u32[]{:S(2)}, u32[]{:S(2)}) collective-permute-start(f32[128]{0:T(128)S(1)} %multiply_reduce_fusion), channel_id=1, source_target_pairs={{0,1},{1,0},{2,3},{3,2},{4,5},{5,4},{6,7},{7,6},{8,9},{9,8},{10,11... | collective-permute-start | bytes 1544 | tf_op jit(solution)/shard_map/ppermute | solution.py:18
  106.5 2.0 %collective-permute-done.23 = f32[128]{0:T(128)S(1)} collective-permute-done((f32[128]{0:T(128)S(1)}, f32[128]{0:T(128)S(1)}, u32[]{:S(2)}, u32[]{:S(2)}) %collective-permute-start.23) | collective-permute-done | bytes 544 | tf_op jit(solution)/shard_map/ppermute | solution.py:18
  (82 shorter events, 16.6 us)
Async XLA Ops:
  0.9 14.2 %collective-permute-start.2 = (bf16[128,512]{1,0:T(8,128)(2,1)S(1)}, bf16[128,512]{1,0:T(8,128)(2,1)S(1)}, u32[]{:S(2)}, u32[]{:S(2)}) collective-permute-start(bf16[128,512]{1,0:T(8,128)(2,1)S(1)} %constant_dynamic-update-slice_fusion), channel_id=1, source_target_pairs={{0,4},{2,6},{4,0},{6,2},{8,12},{10,14},{12,8},{14,10},{16,20},{18,... | collective-permute-start | bytes 393224 | tf_op jit(solution)/shard_map/ppermute | solution.py:18
  3.9 8.0 %collective-permute-start.1 = (bf16[128,512]{1,0:T(8,128)(2,1)S(1)}, bf16[128,512]{1,0:T(8,128)(2,1)S(1)}, u32[]{:S(2)}, u32[]{:S(2)}) collective-permute-start(bf16[128,512]{1,0:T(8,128)(2,1)S(1)} %constant_dynamic-update-slice_fusion), channel_id=1, source_target_pairs={{0,16},{2,18},{4,20},{6,22},{8,24},{10,26},{12,28},{14,30},{1,17},... | collective-permute-start | bytes 393224 | tf_op jit(solution)/shard_map/ppermute | solution.py:24
  8.4 6.0 %collective-permute-start = (bf16[128,512]{1,0:T(8,128)(2,1)S(1)}, bf16[128,512]{1,0:T(8,128)(2,1)S(1)}, u32[]{:S(2)}, u32[]{:S(2)}) collective-permute-start(bf16[128,512]{1,0:T(8,128)(2,1)S(1)} %constant_dynamic-update-slice_fusion), channel_id=1, source_target_pairs={{0,8},{2,10},{4,12},{6,14},{8,16},{10,18},{12,20},{14,22},{16,24},... | collective-permute-start | bytes 393224 | tf_op jit(solution)/shard_map/ppermute | solution.py:24
  14.5 6.7 %collective-permute-start.3 = (bf16[2,128,512]{2,1,0:T(8,128)(2,1)S(1)}, bf16[2,128,512]{2,1,0:T(8,128)(2,1)S(1)}, u32[]{:S(2)}, u32[]{:S(2)}) collective-permute-start(bf16[2,128,512]{2,1,0:T(8,128)(2,1)S(1)} %pad_maximum_fusion), channel_id=1, source_target_pairs={{0,4},{2,6},{4,0},{6,2},{8,12},{10,14},{12,8},{14,10},{16,20},{18,... | collective-permute-start | bytes 786440 | tf_op jit(solution)/shard_map/ppermute | solution.py:18
  21.2 8.8 %collective-permute-start.4 = (bf16[6,128,512]{2,1,0:T(8,128)(2,1)S(1)}, bf16[6,128,512]{2,1,0:T(8,128)(2,1)S(1)}, u32[]{:S(2)}, u32[]{:S(2)}) collective-permute-start(bf16[6,128,512]{2,1,0:T(8,128)(2,1)S(1)} %constant_dynamic-update-slice_fusion.2.a_ref), channel_id=1, source_target_pairs={{0,2},{2,0},{4,6},{6,4},{8,10},{10,8},{12,14},{14,12},{16,18},{18,... | collective-permute-start | bytes 2359304 | tf_op jit(solution)/shard_map/ppermute | solution.py:18
  22.1 31.9 %collective-permute-start.14 = (bf16[2048,128]{1,0:T(8,128)(2,1)}, bf16[2048,128]{1,0:T(8,128)(2,1)}, u32[]{:S(2)}, u32[]{:S(2)}) collective-permute-start(bf16[2048,128]{1,0:T(8,128)(2,1)} %slice.90), channel_id=1, source_target_pairs={{0,16},{2,18},{4,20},{6,22},{8,24},{10,26},{12,28},{14,30},{16,0},... | collective-permute-start | bytes 1572872 | tf_op jit(solution)/shard_map/ppermute | solution.py:18
  34.3 30.7 %collective-permute-start.6 = (bf16[128,2048]{1,0:T(8,128)(2,1)S(1)}, bf16[128,2048]{1,0:T(8,128)(2,1)S(1)}, u32[]{:S(2)}, u32[]{:S(2)}) collective-permute-start(bf16[128,2048]{1,0:T(8,128)(2,1)S(1)} %attend.1.refs_0_), channel_id=1, source_target_pairs={{0,8},{2,10},{4,12},{6,14},{8,0},{10,2},{12,4},{14,6},{16,24},{18,... | collective-permute-start | bytes 1572872 | tf_op jit(solution)/shard_map/ppermute | solution.py:18
  35.6 46.8 %collective-permute-start.12 = (bf16[2048,256]{1,0:T(8,128)(2,1)S(1)}, bf16[2048,256]{1,0:T(8,128)(2,1)}, u32[]{:S(2)}, u32[]{:S(2)}) collective-permute-start(bf16[2048,256]{1,0:T(8,128)(2,1)S(1)} %copy-done.1), channel_id=1, source_target_pairs={{0,2},{2,0},{4,6},{6,4},{8,10},{10,8},{12,14},{14,12},{16,18},{18,... | collective-permute-start | bytes 3145736 | tf_op jit(solution)/shard_map/ppermute | solution.py:18
  36.4 30.3 %collective-permute-start.9 = (bf16[1024,128]{1,0:T(8,128)(2,1)}, bf16[1024,128]{1,0:T(8,128)(2,1)S(1)}, u32[]{:S(2)}, u32[]{:S(2)}) collective-permute-start(bf16[1024,128]{1,0:T(8,128)(2,1)} %get-tuple-element.15), channel_id=1, source_target_pairs={{0,16},{2,18},{4,20},{6,22},{8,24},{10,26},{12,28},{14,30},{16,0},... | collective-permute-start | bytes 786440 | tf_op jit(solution)/shard_map/ppermute | solution.py:18
  54.0 26.4 %collective-permute-start.15 = (bf16[2048,128]{1,0:T(8,128)(2,1)}, bf16[2048,128]{1,0:T(8,128)(2,1)}, u32[]{:S(2)}, u32[]{:S(2)}) collective-permute-start(bf16[2048,128]{1,0:T(8,128)(2,1)} %collective-permute-done.14.refs_4_), channel_id=1, source_target_pairs={{0,2},{2,0},{4,6},{6,4},{8,10},{10,8},{12,14},{14,12},{16,18},{18,... | collective-permute-start | bytes 1572872 | tf_op jit(solution)/shard_map/ppermute | solution.py:18
  54.0 25.9 %collective-permute-start.5 = (bf16[128,2048]{1,0:T(8,128)(2,1)S(1)}, bf16[128,2048]{1,0:T(8,128)(2,1)S(1)}, u32[]{:S(2)}, u32[]{:S(2)}) collective-permute-start(bf16[128,2048]{1,0:T(8,128)(2,1)S(1)} %attend.1.refs_0_), channel_id=1, source_target_pairs={{0,4},{2,6},{4,0},{6,2},{8,12},{10,14},{12,8},{14,10},{16,20},{18,... | collective-permute-start | bytes 1572872 | tf_op jit(solution)/shard_map/ppermute | solution.py:18
  65.0 15.5 %collective-permute-start.7 = (bf16[128,2048]{1,0:T(8,128)(2,1)S(1)}, bf16[128,2048]{1,0:T(8,128)(2,1)S(1)}, u32[]{:S(2)}, u32[]{:S(2)}) collective-permute-start(bf16[128,2048]{1,0:T(8,128)(2,1)S(1)} %collective-permute-done.6.refs_2_), channel_id=1, source_target_pairs={{0,4},{2,6},{4,0},{6,2},{8,12},{10,14},{12,8},{14,10},{16,20},{18,... | collective-permute-start | bytes 1572872 | tf_op jit(solution)/shard_map/ppermute | solution.py:18
  66.7 13.2 %collective-permute-start.8 = (bf16[1024,128]{1,0:T(8,128)(2,1)}, bf16[1024,128]{1,0:T(8,128)(2,1)}, u32[]{:S(2)}, u32[]{:S(2)}) collective-permute-start(bf16[1024,128]{1,0:T(8,128)(2,1)} %get-tuple-element.16), channel_id=1, source_target_pairs={{0,16},{2,18},{4,20},{6,22},{8,24},{10,26},{12,28},{14,30},{16,0},... | collective-permute-start | bytes 786440 | tf_op jit(solution)/shard_map/ppermute | solution.py:18
  79.9 8.0 %collective-permute-start.11 = (bf16[1024,128]{1,0:T(8,128)(2,1)S(1)}, bf16[1024,128]{1,0:T(8,128)(2,1)S(1)}, u32[]{:S(2)}, u32[]{:S(2)}) collective-permute-start(bf16[1024,128]{1,0:T(8,128)(2,1)S(1)} %collective-permute-done.9.refs_5_), channel_id=1, source_target_pairs={{0,2},{2,0},{4,6},{6,4},{8,10},{10,8},{12,14},{14,12},{16,18},{18,... | collective-permute-start | bytes 786440 | tf_op jit(solution)/shard_map/ppermute | solution.py:18
  79.9 8.0 %collective-permute-start.10 = (bf16[1024,128]{1,0:T(8,128)(2,1)}, bf16[1024,128]{1,0:T(8,128)(2,1)S(1)}, u32[]{:S(2)}, u32[]{:S(2)}) collective-permute-start(bf16[1024,128]{1,0:T(8,128)(2,1)} %collective-permute-done.8.refs_4_), channel_id=1, source_target_pairs={{0,2},{2,0},{4,6},{6,4},{8,10},{10,8},{12,14},{14,12},{16,18},{18,... | collective-permute-start | bytes 786440 | tf_op jit(solution)/shard_map/ppermute | solution.py:18
  84.3 8.9 %collective-permute-start.16 = (bf16[512,256]{1,0:T(8,128)(2,1)S(1)}, bf16[512,256]{1,0:T(8,128)(2,1)S(1)}, u32[]{:S(2)}, u32[]{:S(2)}) collective-permute-start(bf16[512,256]{1,0:T(8,128)(2,1)S(1)} %broadcast_select_fusion), channel_id=1, source_target_pairs={{0,1},{1,0},{2,3},{3,2},{4,5},{5,4},{6,7},{7,6},{8,9},{9,8},{10,11... | collective-permute-start | bytes 786440 | tf_op jit(solution)/shard_map/ppermute | solution.py:18
  89.6 8.6 %collective-permute-start.13 = (bf16[512,256]{1,0:T(8,128)(2,1)S(1)}, bf16[512,256]{1,0:T(8,128)(2,1)S(1)}, u32[]{:S(2)}, u32[]{:S(2)}) collective-permute-start(bf16[512,256]{1,0:T(8,128)(2,1)S(1)} %broadcast_select_fusion.1), channel_id=1, source_target_pairs={{0,1},{1,0},{2,3},{3,2},{4,5},{5,4},{6,7},{7,6},{8,9},{9,8},{10,11... | collective-permute-start | bytes 786440 | tf_op jit(solution)/shard_map/ppermute | solution.py:18
  93.4 6.8 %collective-permute-start.20 = (bf16[128,256]{1,0:T(8,128)(2,1)S(1)}, bf16[128,256]{1,0:T(8,128)(2,1)S(1)}, u32[]{:S(2)}, u32[]{:S(2)}) collective-permute-start(bf16[128,256]{1,0:T(8,128)(2,1)S(1)} %get-tuple-element.24), channel_id=1, source_target_pairs={{0,8},{2,10},{4,12},{6,14},{8,0},{10,2},{12,4},{14,6},{16,24},{18,... | collective-permute-start | bytes 196616 | tf_op jit(solution)/shard_map/ppermute | solution.py:18
  93.5 8.6 %collective-permute-start.22 = (bf16[128,256]{1,0:T(8,128)(2,1)S(1)}, bf16[128,256]{1,0:T(8,128)(2,1)S(1)}, u32[]{:S(2)}, u32[]{:S(2)}) collective-permute-start(bf16[128,256]{1,0:T(8,128)(2,1)S(1)} %get-tuple-element.25), channel_id=1, source_target_pairs={{0,12},{2,14},{4,8},{6,10},{8,4},{10,6},{12,0},{14,2},{16,28},{18,... | collective-permute-start | bytes 196616 | tf_op jit(solution)/shard_map/ppermute | solution.py:18
  95.2 8.6 %collective-permute-start.18 = (bf16[128,256]{1,0:T(8,128)(2,1)S(1)}, bf16[128,256]{1,0:T(8,128)(2,1)S(1)}, u32[]{:S(2)}, u32[]{:S(2)}) collective-permute-start(bf16[128,256]{1,0:T(8,128)(2,1)S(1)} %get-tuple-element.26), channel_id=1, source_target_pairs={{0,4},{2,6},{4,0},{6,2},{8,12},{10,14},{12,8},{14,10},{16,20},{18,... | collective-permute-start | bytes 196616 | tf_op jit(solution)/shard_map/ppermute | solution.py:18
  98.4 4.3 %collective-permute-start.19 = (bf16[128,256]{1,0:T(8,128)(2,1)S(1)}, bf16[128,256]{1,0:T(8,128)(2,1)S(1)}, u32[]{:S(2)}, u32[]{:S(2)}) collective-permute-start(bf16[128,256]{1,0:T(8,128)(2,1)S(1)} %get-tuple-element.21), channel_id=1, source_target_pairs={{0,8},{2,10},{4,12},{6,14},{8,0},{10,2},{12,4},{14,6},{16,24},{18,... | collective-permute-start | bytes 196616 | tf_op jit(solution)/shard_map/ppermute | solution.py:18
  98.4 5.2 %collective-permute-start.21 = (bf16[128,256]{1,0:T(8,128)(2,1)S(1)}, bf16[128,256]{1,0:T(8,128)(2,1)S(1)}, u32[]{:S(2)}, u32[]{:S(2)}) collective-permute-start(bf16[128,256]{1,0:T(8,128)(2,1)S(1)} %get-tuple-element.22), channel_id=1, source_target_pairs={{0,12},{2,14},{4,8},{6,10},{8,4},{10,6},{12,0},{14,2},{16,28},{18,... | collective-permute-start | bytes 196616 | tf_op jit(solution)/shard_map/ppermute | solution.py:18
  100.2 4.3 %collective-permute-start.17 = (bf16[128,256]{1,0:T(8,128)(2,1)S(1)}, bf16[128,256]{1,0:T(8,128)(2,1)S(1)}, u32[]{:S(2)}, u32[]{:S(2)}) collective-permute-start(bf16[128,256]{1,0:T(8,128)(2,1)S(1)} %get-tuple-element.23), channel_id=1, source_target_pairs={{0,4},{2,6},{4,0},{6,2},{8,12},{10,14},{12,8},{14,10},{16,20},{18,... | collective-permute-start | bytes 196616 | tf_op jit(solution)/shard_map/ppermute | solution.py:18
  104.9 3.6 %collective-permute-start.23 = (f32[128]{0:T(128)S(1)}, f32[128]{0:T(128)S(1)}, u32[]{:S(2)}, u32[]{:S(2)}) collective-permute-start(f32[128]{0:T(128)S(1)} %multiply_reduce_fusion), channel_id=1, source_target_pairs={{0,1},{1,0},{2,3},{3,2},{4,5},{5,4},{6,7},{7,6},{8,9},{9,8},{10,11... | collective-permute-start | bytes 1544 | tf_op jit(solution)/shard_map/ppermute | solution.py:18
  (7 other events, 93.6 us)
where the time goes:
time: 110 us
  waiting for transfers between devices  53.3 us (48%)
  starting transfers between devices  36.1 us (33%)
  Pallas kernels  10.7 us (10%)
  local copies, waits for them, and re-layouts  5.2 us (5%)
  other arithmetic  3.28 us (3%)
    ppermute x22, waiting for transfers between devices, flipped(): return lax.ppermute(block, axis, [(i, i ^ mask) for i in devices])  50.9 us
    ppermute x22, starting transfers between devices, flipped(): return lax.ppermute(block, axis, [(i, i ^ mask) for i in devices])  28.2 us
    ppermute x2, starting transfers between devices, shifted(): return lax.ppermute(block, axis, route)  7.98 us
    pallas_call x4, Pallas kernels, project(): pl.pallas_call(functools.partial(project_kernel, len(rows), tuple(layout)...  7.43 us
    unnamed x19, local copies, waits for them, and re-layouts  3.3 us
    pallas_call x1, Pallas kernels, attend(): pl.pallas_call(functools.partial(attention_kernel, kv_heads, groups), out...  3.26 us
    ppermute x2, waiting for transfers between devices, shifted(): return lax.ppermute(block, axis, route)  2.47 us
  transfers between devices with their start and end apart: 24, of which 11 were waited for; matrix products, arithmetic and copies ran while one was open for 4% of the time, Pallas kernels for 10%

commit v1 on v0

v1 whole, which is shorter than its diff:
```python
import functools
import jax
import jax.numpy as jnp
from jax import lax
from jax.experimental import pallas as pl
from jax.experimental.pallas import tpu as pltpu
from jax.sharding import PartitionSpec as P


HEAD_SIZE = 128
BLK = 16
LOW_BITS = 2
FIRST_STRETCHES = (3, 1)


def flipped(block, mask, axis="srv"):
    devices = range(lax.axis_size(axis))
    return lax.ppermute(block, axis, [(i, i ^ mask) for i in devices])


def shifted(block, axis, distance):
    devices = range(lax.axis_size(axis))
    route = [(i - distance, i) for i in devices if i - distance in devices]
    return lax.ppermute(block, axis, route)


def attention_kernel(kv_heads, h, info, q_ref, a_ref, b_ref, o_ref, s_s, m_s, l_s, acc_s):
    groups, rows, _ = q_ref.shape
    pairs = a_ref.shape[0]
    docs = info.shape[0] - 1 - 2 * pairs
    scale = HEAD_SIZE ** (-0.5)
    base = info[0]
    position = base + lax.broadcasted_iota(jnp.int32, (rows, 2 * rows), 0)
    first = jnp.zeros((rows, 2 * rows), jnp.int32)
    lowest = jnp.int32(0)
    begin = jnp.int32(0)
    for d in range(docs):
        end = begin + info[1 + 2 * pairs + d] * BLK
        first = jnp.where((position >= begin) & (position < end), begin, first)
        lowest = jnp.where((base >= begin) & (base < end), begin, lowest)
        begin = end
    limit = (position // BLK + 1) * BLK
    lane = lax.broadcasted_iota(jnp.int32, (rows, 2 * rows), 1)
    k_at = h * HEAD_SIZE
    v_at = (kv_heads + h) * HEAD_SIZE
    m_s[...] = jnp.full(m_s.shape, -1e30, jnp.float32)
    l_s[...] = jnp.zeros(l_s.shape, jnp.float32)
    acc_s[...] = jnp.zeros(acc_s.shape, jnp.float32)

    def active(p):
        low = jnp.minimum(info[1 + 2 * p], info[2 + 2 * p])
        return (low + 2 * rows > lowest) & (low < base + rows)

    def score(p, carry):
        @pl.when(active(p))
        def _():
            k = jnp.concatenate(
                [a_ref[p, :, k_at : k_at + HEAD_SIZE], b_ref[p, :, k_at : k_at + HEAD_SIZE]], 0
            )
            key_pos = jnp.where(lane < rows, info[1 + 2 * p] + lane, info[2 + 2 * p] + lane - rows)
            mask = (key_pos >= first) & (key_pos < limit)
            for g in range(groups):
                s = lax.dot_general(
                    q_ref[g], k, (((1,), (1,)), ((), ())), preferred_element_type=jnp.float32
                )
                s = jnp.where(mask, s * scale, -1e30)
                s_s[p, g] = s
                m_s[g] = jnp.maximum(m_s[g], jnp.maximum(s[:, :rows], s[:, rows:]))

        return carry

    lax.fori_loop(0, pairs, score, 0)
    for g in range(groups):
        m_s[g] = jnp.broadcast_to(jnp.max(m_s[g], axis=1, keepdims=True), (rows, rows))

    def weigh(p, carry):
        @pl.when(active(p))
        def _():
            v = jnp.concatenate(
                [a_ref[p, :, v_at : v_at + HEAD_SIZE], b_ref[p, :, v_at : v_at + HEAD_SIZE]], 0
            )
            for g in range(groups):
                m = m_s[g]
                w = jnp.exp(s_s[p, g] - jnp.concatenate([m, m], 1))
                l_s[g] += w[:, :rows] + w[:, rows:]
                acc_s[g] += jnp.dot(w.astype(jnp.bfloat16), v, preferred_element_type=jnp.float32)

        return carry

    lax.fori_loop(0, pairs, weigh, 0)
    for g in range(groups):
        at = g * HEAD_SIZE
        total = jnp.sum(l_s[g], axis=1, keepdims=True)
        o_ref[:, at : at + HEAD_SIZE] = (acc_s[g] / total).astype(o_ref.dtype)


def attend(info, queries, near, far, kv_heads, h):
    groups, rows, _ = queries.shape
    pairs = near.shape[0]
    vmem = pl.BlockSpec(memory_space=pltpu.VMEM)
    return pl.pallas_call(
        functools.partial(attention_kernel, kv_heads, h),
        out_shape=jax.ShapeDtypeStruct((rows, groups * HEAD_SIZE), jnp.bfloat16),
        in_specs=[pl.BlockSpec(memory_space=pltpu.SMEM), vmem, vmem, vmem],
        out_specs=vmem,
        scratch_shapes=[
            pltpu.VMEM((pairs, groups, rows, 2 * rows), jnp.float32),
            pltpu.VMEM((groups, rows, rows), jnp.float32),
            pltpu.VMEM((groups, rows, rows), jnp.float32),
            pltpu.VMEM((groups, rows, HEAD_SIZE), jnp.float32),
        ],
        cost_estimate=pl.CostEstimate(
            flops=8 * rows * groups * HEAD_SIZE * pairs * rows,
            bytes_accessed=4 * rows * groups * HEAD_SIZE,
            transcendentals=2 * rows * rows * pairs * groups,
        ),
        compiler_params=pltpu.CompilerParams(vmem_limit_bytes=32 * 1024 * 1024),
        name="attend",
    )(info, queries, near, far)


def ordered(parts, bit):
    low = jnp.concatenate(parts, axis=-1)
    high = jnp.concatenate(parts[::-1], axis=-1)
    return jnp.where(bit == 0, low, high)


def project_kernel(count, halves, layout, cut, *refs):
    rows = [refs[i * halves : (i + 1) * halves] for i in range(count)]
    arrays = refs[count * halves : -1]
    out = refs[-1]
    columns = []
    for segments in layout:
        taken = [arrays[n][:, at : at + cut] for n, at in segments]
        columns.append(taken[0] if len(taken) == 1 else jnp.concatenate(taken, axis=0))
    w = columns[0] if len(columns) == 1 else jnp.concatenate(columns, axis=1)
    size = rows[0][0].shape[0]
    for i in range(count):
        x = jnp.concatenate([r[...] for r in rows[i]], axis=1)
        out[i * size : (i + 1) * size, :] = jnp.dot(
            x, w, preferred_element_type=jnp.float32
        ).astype(out.dtype)


def project(rows, parts, cut):
    halves = len(rows[0])
    height = sum(r[0].shape[0] for r in rows)
    depth = sum(x.shape[1] for x in rows[0])
    width = cut * len(parts)
    flat = [x for r in rows for x in r]
    if cut % 128:
        columns = [
            jnp.concatenate([w[:, at : at + cut] for w, at in segments], 0) for segments in parts
        ]
        joined = jnp.dot(
            jnp.concatenate([jnp.concatenate(r, 1) for r in rows], 0),
            jnp.concatenate(columns, 1),
            preferred_element_type=jnp.float32,
        )
        return joined.astype(jnp.bfloat16)
    arrays = [w for segments in parts for w, _ in segments]
    layout, n = [], 0
    for segments in parts:
        layout.append(tuple((n + i, at) for i, (_, at) in enumerate(segments)))
        n += len(segments)
    vmem = pl.BlockSpec(memory_space=pltpu.VMEM)
    return pl.pallas_call(
        functools.partial(project_kernel, len(rows), halves, tuple(layout), cut),
        out_shape=jax.ShapeDtypeStruct((height, width), jnp.bfloat16),
        in_specs=[vmem] * (len(flat) + len(arrays)),
        out_specs=vmem,
        cost_estimate=pl.CostEstimate(
            flops=2 * height * width * depth,
            bytes_accessed=2 * depth * (height + width),
            transcendentals=0,
        ),
        compiler_params=pltpu.CompilerParams(vmem_limit_bytes=24 * 1024 * 1024),
        name="project",
    )(*flat, *arrays)


def on_device(
    queries, keys, values, residual, out_weight, norm_gain, level_shift, doc_lengths, noise_level
):
    rows = queries.shape[0]
    here = lax.axis_index("srv")
    devices = lax.axis_size("srv")
    sections = lax.axis_size("section")
    peers = lax.axis_size("tp")
    mine = lax.axis_index("tp")
    whole_index = lax.axis_index("section") * devices + here
    bits = devices.bit_length() - 1
    low = 1 << LOW_BITS
    width = out_weight.shape[1]
    chunks = max(1, width // 128)
    cut = width // chunks

    kv = jnp.concatenate([keys, values], axis=1)
    turns = -(-(devices // 2) // low)
    back = []
    for k in range(1, turns + 1):
        back.append(shifted(kv, "srv", low * k))
    beside = flipped(kv, 2)
    beside_back = flipped(jnp.stack(back), 2)
    own = here % low
    block = here - own
    order = [(k, 0) for k in range(turns + 1)] + [(k, 2) for k in range(turns + 1)]
    spots = []
    for k, x in order:
        for c in (0, 1):
            spots.append((block - low * k + (own ^ (x + c))) * rows)
    info = jnp.stack([here * rows] + spots).astype(jnp.int32)
    info = jnp.concatenate([info, doc_lengths[0].astype(jnp.int32)])
    by_head = queries.reshape(rows, -1, HEAD_SIZE).transpose(1, 0, 2)
    beside_back, by_head, info = lax.optimization_barrier((beside_back, by_head, info))
    near = jnp.concatenate([jnp.stack([kv] + back + [beside]), beside_back], axis=0)
    far = flipped(near, 1)

    depth = out_weight.shape[0]
    pieces_of = []
    for j in range(chunks):
        shares = FIRST_STRETCHES if j == 0 else (1,)
        unit = depth // sum(shares)
        pieces_of.append([(n, sum(shares[:n]) * unit, share * unit) for n, share in enumerate(shares)])
    held = []
    for j in range(chunks):
        segments = []
        for n, at, size in pieces_of[j]:
            got = {0: out_weight[at : at + size, j * cut : (j + 1) * cut]}
            for b in range(3, bits):
                got.update({r | (1 << b): flipped(w, 1 << b) for r, w in list(got.items())})
            hop = 1
            while hop < sections:
                got.update(
                    {r | (hop * devices): flipped(w, hop, "section") for r, w in list(got.items())}
                )
                hop *= 2
            segments.append(got)
        held.append(segments)
    beside_own = flipped(out_weight, 1)
    sources = []
    for j in range(chunks):
        found = {0: [(out_weight, j * cut)], 1: [(beside_own, j * cut)]}
        for got in held[j]:
            for r, w in got.items():
                if r:
                    found.setdefault(r, []).append((w, 0))
                    found.setdefault(r | 1, []).append((flipped(w, 1), 0))
        sources.append(found)

    kv_heads = keys.shape[1] // HEAD_SIZE
    groups = by_head.shape[0] // kv_heads
    attended, across = [], []
    for h in range(kv_heads):
        attended.append(
            attend(info, by_head[h * groups : (h + 1) * groups], near, far, kv_heads, h)
        )
        across.append(flipped(attended[h], 4))
    row_keys = (0, 2, 4, 6)
    beside_rows, cross_rows = [], []
    for h in range(kv_heads):
        beside_rows.append(flipped(attended[h], 2))
        cross_rows.append(flipped(across[h], 2))
    gathered = [attended, beside_rows, across, cross_rows]

    lengths = doc_lengths[0] * BLK
    ends = jnp.cumsum(lengths)
    starts = ends - lengths
    positions = here * rows + jnp.arange(rows, dtype=jnp.int32)
    member = (positions[:, None] >= starts[None, :]) & (positions[:, None] < ends[None, :])
    level = jnp.sum(jnp.where(member, noise_level[0][None, :], 0), axis=1)
    onehot = (level[:, None] == jnp.arange(level_shift.shape[0], dtype=jnp.int32)[None, :]).astype(
        jnp.float32
    )
    shift = jnp.dot(onehot, level_shift, precision=lax.Precision.HIGHEST)
    factor = norm_gain[None, :] * (1.0 + shift)
    blocks = residual.shape[1] // width
    residuals = [
        jnp.concatenate(
            [residual[:, b * width + j * cut : b * width + (j + 1) * cut] for b in range(blocks)], 1
        )
        for j in range(chunks)
    ]
    factor, residuals, beside_rows[0] = lax.optimization_barrier(
        (factor, residuals, beside_rows[0])
    )

    span = sections * devices // peers
    turn = whole_index // span ^ mine
    lower = sorted(r for r in sources[0] if r < span)
    hidden, squares = [], 0.0
    for j in range(chunks):
        by_part = []
        pieces = {}
        for part in range(peers):
            by_part.append(
                project(gathered, [sources[j][part * span + r] for r in lower], cut)
            )

        def chosen(e):
            value = by_part[0]
            for part in range(1, peers):
                value = jnp.where((turn ^ e) == part, by_part[part], value)
            return value

        total = chosen(0).astype(jnp.float32)
        for e in range(1, peers):
            total = total + flipped(chosen(e), e, "tp").astype(jnp.float32)
        for i, r in enumerate(row_keys):
            piece = total[i * rows : (i + 1) * rows]
            if r:
                piece = flipped(piece.astype(jnp.bfloat16), r).astype(jnp.float32)
            for n, a in enumerate(lower):
                pieces[a ^ r] = piece[:, n * cut : (n + 1) * cut]
        b = 1
        while len(pieces) > 1:
            pieces = {
                r: ordered([pieces[r], pieces[r | b]], (whole_index // b) % 2)
                for r in pieces
                if not r & b
            }
            b *= 2
        hidden.append(pieces[0] + residuals[j].astype(jnp.float32))
        squares = squares + jnp.sum(hidden[j] * hidden[j], axis=1)

    hop = 1
    while hop < peers:
        squares = squares + flipped(squares, hop, "tp")
        hop *= 2
    inverse = lax.rsqrt(squares / (residual.shape[1] * peers) + 1e-06)[:, None]
    normed = jnp.concatenate(
        [hidden[j][:, b * cut : (b + 1) * cut] for b in range(blocks) for j in range(chunks)], axis=1
    )
    return (normed * inverse * factor).astype(jnp.bfloat16)


def solution(mesh):
    placed = (
        P(("section", "srv"), "tp"),
        P(("section", "srv"), "tp"),
        P(("section", "srv"), "tp"),
        P(("section", "srv"), "tp"),
        P("tp", ("section", "srv")),
        P("tp"),
        P(None, "tp"),
        P("section", None),
        P("section", None),
    )
    return jax.shard_map(
        on_device,
        mesh=mesh,
        in_specs=placed,
        out_specs=P(("section", "srv"), "tp"),
        check_vma=False,
    )
```

time: 110 us -> 139 us (1.26)
  local copies, waits for them, and re-layouts: 5.2 us -> 27.7 us
  waiting for transfers between devices: 53.3 us -> 60.2 us
  starting transfers between devices: 36.1 us -> 33.1 us
  Pallas kernels: 10.7 us -> 12.9 us
    unnamed x19 -> x52, local copies, waits for them, and re-layouts: 3.3 us -> 18 us
    ppermute x22 -> x25, waiting for transfers between devices: 50.9 us -> 60.2 us  [flipped(): return lax.ppermute(block, axis, [(i, i ^ mask) for i in devices])]
    slice x10 -> x12, local copies, waits for them, and re-layouts: 1.76 us -> 5.42 us  [the longest x3 4.17 us: on_device(): got = {0: out_weight[at:at + size, j * cut:(j + 1) * cut]}]
    ppermute x22 -> x25, starting transfers between devices: 28.2 us -> 25.1 us  [flipped(): return lax.ppermute(block, axis, [(i, i ^ mask) for i in devices])]
    ppermute x2, waiting for transfers between devices: 2.47 us -> 0.01 us  [shifted(): return lax.ppermute(block, axis, route)]
    pallas_call x5 -> x6, Pallas kernels: 10.7 us -> 12.9 us  [the longest x4 7.76 us: project(): pl.pallas_call(functools.partial(project_kernel, len(rows), halves, tuple...]
    reshape x0 -> x1, local copies, waits for them, and re-layouts: none -> 2.05 us  [on_device(): by_head = queries.reshape(rows, -1, HEAD_SIZE).transpose(1, 0, 2)]
    concatenate x0 -> x2, local copies, waits for them, and re-layouts: none -> 1.41 us  [the longest x1 1.4 us: on_device(): jnp.concatenate([residual[:, b * width + j * cut:b * width + (j + 1) * cu...]
  transfers between devices with their start and end apart: 24 -> 27, of which waited for: 11 -> 12; matrix products, arithmetic and copies ran while one was open for 4% -> 16% of each run, Pallas kernels for 10% -> 9%
where the time goes in v1:
time: 139 us; the launch traced here: 137 us
  waiting for transfers between devices  60.2 us (43%)
  starting transfers between devices  33.1 us (24%)
  local copies, waits for them, and re-layouts  27.7 us (20%)
  Pallas kernels  12.9 us (9%)
  other arithmetic  2.09 us (2%)
    ppermute x25, waiting for transfers between devices, flipped(): return lax.ppermute(block, axis, [(i, i ^ mask) for i in devices])  60.2 us
    ppermute x25, starting transfers between devices, flipped(): return lax.ppermute(block, axis, [(i, i ^ mask) for i in devices])  25.1 us
    unnamed x52, local copies, waits for them, and re-layouts  18 us
    ppermute x2, starting transfers between devices, shifted(): return lax.ppermute(block, axis, route)  7.98 us
    pallas_call x4, Pallas kernels, project(): pl.pallas_call(functools.partial(project_kernel, len(rows), halves, tuple...  7.76 us
    pallas_call x2, Pallas kernels, attend(): pl.pallas_call(functools.partial(attention_kernel, kv_heads, h), out_shap...  5.13 us
    slice x3, local copies, waits for them, and re-layouts, on_device(): got = {0: out_weight[at:at + size, j * cut:(j + 1) * cut]}  4.17 us
  transfers between devices with their start and end apart: 27, of which 12 were waited for; matrix products, arithmetic and copies ran while one was open for 16% of the time, Pallas kernels for 9%

profile of v1, /device:TPU:0, one launch (start us, length us, event | category | flops | bytes accessed | tf_op | source)
XLA Modules:
  0.0 137.3 jit_solution(14309254585777316850)
XLA Ops:
  2.2 3.0 %collective-permute-start.3 = (bf16[128,512]{1,0:T(8,128)(2,1)}, bf16[128,512]{1,0:T(8,128)(2,1)}, u32[]{:S(2)}, u32[]{:S(2)}) collective-permute-start(bf16[128,512]{1,0:T(8,128)(2,1)} %constant_dynamic-update-slice_fusion), channel_id=1, source_target_pairs={{0,4},{2,6},{4,0},{6,2},{8,12},{10,14},{12,8},{14,10},{16,20},{18,... | collective-permute-start | bytes 393224 | tf_op jit(solution)/shard_map/ppermute | solution.py:18
  5.2 4.5 %collective-permute-start.1 = (bf16[128,512]{1,0:T(8,128)(2,1)}, bf16[128,512]{1,0:T(8,128)(2,1)S(1)}, u32[]{:S(2)}, u32[]{:S(2)}) collective-permute-start(bf16[128,512]{1,0:T(8,128)(2,1)} %constant_dynamic-update-slice_fusion), channel_id=1, source_target_pairs={{0,16},{2,18},{4,20},{6,22},{8,24},{10,26},{12,28},{14,30},{1,17},... | collective-permute-start | bytes 393224 | tf_op jit(solution)/shard_map/ppermute | solution.py:24
  9.7 3.5 %collective-permute-start = (bf16[128,512]{1,0:T(8,128)(2,1)}, bf16[128,512]{1,0:T(8,128)(2,1)S(1)}, u32[]{:S(2)}, u32[]{:S(2)}) collective-permute-start(bf16[128,512]{1,0:T(8,128)(2,1)} %constant_dynamic-update-slice_fusion), channel_id=1, source_target_pairs={{0,8},{2,10},{4,12},{6,14},{8,16},{10,18},{12,20},{14,22},{16,24},... | collective-permute-start | bytes 393224 | tf_op jit(solution)/shard_map/ppermute | solution.py:24
  14.8 1.8 %slice.215 = bf16[1536,128]{1,0:T(8,128)(2,1)} slice(bf16[2048,256]{1,0:T(8,128)(2,1)} %refs_8_.3), slice={[0:1536], [0:128]} | slice | bytes 786432 | tf_op jit(solution)/shard_map/slice | solution.py:229
  18.4 2.0 %copy.12 = bf16[128,2048]{0,1:T(8,128)(2,1)} copy(bf16[128,2048]{1,0:T(8,128)(2,1)} %param.9) | data formatting | bytes 1048576 | tf_op args[0]
  20.4 2.0 %copy.13 = bf16[128,16,128]{2,0,1:T(8,128)(2,1)} copy(bf16[128,16,128]{0,2,1:T(8,128)(2,1)} %bitcast.35) | data formatting | bytes 1048576 | tf_op jit(solution)/shard_map/reshape | solution.py:214
  29.3 2.9 %collective-permute-start.11 = (bf16[1536,128]{1,0:T(8,128)(2,1)}, bf16[1536,128]{1,0:T(8,128)(2,1)}, u32[]{:S(2)}, u32[]{:S(2)}) collective-permute-start(bf16[1536,128]{1,0:T(8,128)(2,1)} %slice.215), channel_id=1, source_target_pairs={{0,16},{2,18},{4,20},{6,22},{8,24},{10,26},{12,28},{14,30},{16,0},... | collective-permute-start | bytes 1179656 | tf_op jit(solution)/shard_map/ppermute | solution.py:18
  33.9 6.6 %collective-permute-done.2 = bf16[2,128,512]{2,1,0:T(8,128)(2,1)S(1)} collective-permute-done((bf16[2,128,512]{2,1,0:T(8,128)(2,1)S(1)}, bf16[2,128,512]{2,1,0:T(8,128)(2,1)S(1)}, u32[]{:S(2)}, u32[]{:S(2)}) %collective-permute-start.2) | collective-permute-done | bytes 262176 | tf_op jit(solution)/shard_map/ppermute | solution.py:18
  44.9 27.5 %collective-permute-done.20.refs_8_ = bf16[2048,128]{1,0:T(8,128)(2,1)} collective-permute-done((bf16[2048,128]{1,0:T(8,128)(2,1)}, bf16[2048,128]{1,0:T(8,128)(2,1)}, u32[]{:S(2)}, u32[]{:S(2)}) %collective-permute-start.20) | collective-permute-done | bytes 524320 | tf_op jit(solution)/shard_map/ppermute | solution.py:18
  72.5 2.6 %attend.2.refs_0_ = bf16[128,1024]{1,0:T(8,128)(2,1)S(1)} custom-call(s32[17]{0:T(128)S(1)} %concatenate.91.info, bf16[8,128,128]{2,1,0:T(8,128)(2,1)S(1)} %get-tuple-element.32.q_ref, bf16[6,128,512]{2,1,0:T(8,128)(2,1)S(1)} %constant_dynamic-update-slice_fusion.2.a_ref, bf16[6,128,512]{2,1,0:T(8,128)(2,1)} %collective-permute-done.4.b_ref), custom_call_target="tpu_custom_call" | custom-call | flops 805306368 | bytes 524288 | tf_op jit(solution)/shard_map/attend/pallas_call | solution.py:101
  77.3 2.6 %attend.3.refs_1_ = bf16[128,1024]{1,0:T(8,128)(2,1)S(1)} custom-call(s32[17]{0:T(128)S(1)} %concatenate.91.info, bf16[8,128,128]{2,1,0:T(8,128)(2,1)S(1)} %get-tuple-element.31.q_ref, bf16[6,128,512]{2,1,0:T(8,128)(2,1)S(1)} %copy-done.3, bf16[6,128,512]{2,1,0:T(8,128)(2,1)} %collective-permute-done.4.b_ref), custom_call_target="tpu_custom_call" | custom-call | flops 805306368 | bytes 524288 | tf_op jit(solution)/shard_map/attend/pallas_call | solution.py:101
  80.7 2.0 %collective-permute-start.8 = (bf16[128,1024]{1,0:T(8,128)(2,1)S(1)}, bf16[128,1024]{1,0:T(8,128)(2,1)S(1)}, u32[]{:S(2)}, u32[]{:S(2)}) collective-permute-start(bf16[128,1024]{1,0:T(8,128)(2,1)S(1)} %attend.3.refs_1_), channel_id=1, source_target_pairs={{0,8},{2,10},{4,12},{6,14},{8,0},{10,2},{12,4},{14,6},{16,24},{18,... | collective-permute-start | bytes 786440 | tf_op jit(solution)/shard_map/ppermute | solution.py:18
  84.9 4.2 %collective-permute-done.5.refs_2_ = bf16[128,1024]{1,0:T(8,128)(2,1)S(1)} collective-permute-done((bf16[128,1024]{1,0:T(8,128)(2,1)S(1)}, bf16[128,1024]{1,0:T(8,128)(2,1)S(1)}, u32[]{:S(2)}, u32[]{:S(2)}) %collective-permute-start.5) | collective-permute-done | bytes 262176 | tf_op jit(solution)/shard_map/ppermute | solution.py:18
  94.8 5.6 %collective-permute-done.9.refs_6_ = bf16[128,1024]{1,0:T(8,128)(2,1)} collective-permute-done((bf16[128,1024]{1,0:T(8,128)(2,1)S(1)}, bf16[128,1024]{1,0:T(8,128)(2,1)}, u32[]{:S(2)}, u32[]{:S(2)}) %collective-permute-start.9) | collective-permute-done | bytes 262176 | tf_op jit(solution)/shard_map/ppermute | solution.py:18
  100.4 4.9 %collective-permute-done.10.refs_7_ = bf16[128,1024]{1,0:T(8,128)(2,1)} collective-permute-done((bf16[128,1024]{1,0:T(8,128)(2,1)S(1)}, bf16[128,1024]{1,0:T(8,128)(2,1)}, u32[]{:S(2)}, u32[]{:S(2)}) %collective-permute-start.10) | collective-permute-done | bytes 262176 | tf_op jit(solution)/shard_map/ppermute | solution.py:18
  105.3 2.2 %project.6 = bf16[512,256]{1,0:T(8,128)(2,1)S(1)} custom-call(bf16[128,1024]{1,0:T(8,128)(2,1)S(1)} %attend.2.refs_0_, bf16[128,1024]{1,0:T(8,128)(2,1)S(1)} %attend.3.refs_1_, bf16[128,1024]{1,0:T(8,128)(2,1)S(1)} %collective-permute-done.5.refs_2_, bf16[128,1024]{1,0:T(8,128)(2,1)} %collective-permute-done.6.refs_3_, ...), custom_call_target="tpu_custom_call" | custom-call | flops 536870912 | bytes 3145728 | tf_op jit(solution)/shard_map/project/pallas_call | solution.py:167
  107.5 1.8 %project.7 = bf16[512,256]{1,0:T(8,128)(2,1)S(1)} custom-call(bf16[128,1024]{1,0:T(8,128)(2,1)S(1)} %attend.2.refs_0_, bf16[128,1024]{1,0:T(8,128)(2,1)S(1)} %attend.3.refs_1_, bf16[128,1024]{1,0:T(8,128)(2,1)S(1)} %collective-permute-done.5.refs_2_, bf16[128,1024]{1,0:T(8,128)(2,1)} %collective-permute-done.6.refs_3_, ...), custom_call_target="tpu_custom_call" | custom-call | flops 536870912 | bytes 3145728 | tf_op jit(solution)/shard_map/project/pallas_call | solution.py:167
  110.9 1.8 %project.5 = bf16[512,256]{1,0:T(8,128)(2,1)S(1)} custom-call(bf16[128,1024]{1,0:T(8,128)(2,1)S(1)} %attend.2.refs_0_, bf16[128,1024]{1,0:T(8,128)(2,1)S(1)} %attend.3.refs_1_, bf16[128,1024]{1,0:T(8,128)(2,1)S(1)} %collective-permute-done.5.refs_2_, bf16[128,1024]{1,0:T(8,128)(2,1)} %collective-permute-done.6.refs_3_, ...), custom_call_target="tpu_custom_call" | custom-call | flops 536870912 | bytes 3145728 | tf_op jit(solution)/shard_map/project/pallas_call | solution.py:167
  112.8 2.0 %project.4 = bf16[512,256]{1,0:T(8,128)(2,1)S(1)} custom-call(bf16[128,1024]{1,0:T(8,128)(2,1)S(1)} %attend.2.refs_0_, bf16[128,1024]{1,0:T(8,128)(2,1)S(1)} %attend.3.refs_1_, bf16[128,1024]{1,0:T(8,128)(2,1)S(1)} %collective-permute-done.5.refs_2_, bf16[128,1024]{1,0:T(8,128)(2,1)} %collective-permute-done.6.refs_3_, ...), custom_call_target="tpu_custom_call" | custom-call | flops 536870912 | bytes 3145728 | tf_op jit(solution)/shard_map/project/pallas_call | solution.py:167
  115.4 2.1 %collective-permute-done.22 = bf16[512,256]{1,0:T(8,128)(2,1)S(1)} collective-permute-done((bf16[512,256]{1,0:T(8,128)(2,1)S(1)}, bf16[512,256]{1,0:T(8,128)(2,1)S(1)}, u32[]{:S(2)}, u32[]{:S(2)}) %collective-permute-start.22) | collective-permute-done | bytes 262176 | tf_op jit(solution)/shard_map/ppermute | solution.py:18
  117.6 2.2 %collective-permute-start.24 = (bf16[128,256]{1,0:T(8,128)(2,1)S(1)}, bf16[128,256]{1,0:T(8,128)(2,1)S(1)}, u32[]{:S(2)}, u32[]{:S(2)}) collective-permute-start(bf16[128,256]{1,0:T(8,128)(2,1)S(1)} %get-tuple-element.49), channel_id=1, source_target_pairs={{0,8},{2,10},{4,12},{6,14},{8,0},{10,2},{12,4},{14,6},{16,24},{18,... | collective-permute-start | bytes 196616 | tf_op jit(solution)/shard_map/ppermute | solution.py:18
  122.7 2.2 %collective-permute-start.18 = (bf16[128,256]{1,0:T(8,128)(2,1)S(1)}, bf16[128,256]{1,0:T(8,128)(2,1)S(1)}, u32[]{:S(2)}, u32[]{:S(2)}) collective-permute-start(bf16[128,256]{1,0:T(8,128)(2,1)S(1)} %get-tuple-element.52), channel_id=1, source_target_pairs={{0,8},{2,10},{4,12},{6,14},{8,0},{10,2},{12,4},{14,6},{16,24},{18,... | collective-permute-start | bytes 196616 | tf_op jit(solution)/shard_map/ppermute | solution.py:18
  126.8 3.4 %collective-permute-done.19 = bf16[128,256]{1,0:T(8,128)(2,1)S(1)} collective-permute-done((bf16[128,256]{1,0:T(8,128)(2,1)S(1)}, bf16[128,256]{1,0:T(8,128)(2,1)S(1)}, u32[]{:S(2)}, u32[]{:S(2)}) %collective-permute-start.19) | collective-permute-done | bytes 65568 | tf_op jit(solution)/shard_map/ppermute | solution.py:18
  132.7 1.7 %collective-permute-start.26 = (f32[128]{0:T(128)S(1)}, f32[128]{0:T(128)S(1)}, u32[]{:S(2)}, u32[]{:S(2)}) collective-permute-start(f32[128]{0:T(128)S(1)} %add.128), channel_id=1, source_target_pairs={{0,1},{1,0},{2,3},{3,2},{4,5},{5,4},{6,7},{7,6},{8,9},{9,8},{10,11... | collective-permute-start | bytes 1544 | tf_op jit(solution)/shard_map/ppermute | solution.py:18
  (136 shorter events, 41.6 us)
Async XLA Ops:
  2.2 30.7 %collective-permute-start.3 = (bf16[128,512]{1,0:T(8,128)(2,1)}, bf16[128,512]{1,0:T(8,128)(2,1)}, u32[]{:S(2)}, u32[]{:S(2)}) collective-permute-start(bf16[128,512]{1,0:T(8,128)(2,1)} %constant_dynamic-update-slice_fusion), channel_id=1, source_target_pairs={{0,4},{2,6},{4,0},{6,2},{8,12},{10,14},{12,8},{14,10},{16,20},{18,... | collective-permute-start | bytes 393224 | tf_op jit(solution)/shard_map/ppermute | solution.py:18
  5.2 24.1 %collective-permute-start.1 = (bf16[128,512]{1,0:T(8,128)(2,1)}, bf16[128,512]{1,0:T(8,128)(2,1)S(1)}, u32[]{:S(2)}, u32[]{:S(2)}) collective-permute-start(bf16[128,512]{1,0:T(8,128)(2,1)} %constant_dynamic-update-slice_fusion), channel_id=1, source_target_pairs={{0,16},{2,18},{4,20},{6,22},{8,24},{10,26},{12,28},{14,30},{1,17},... | collective-permute-start | bytes 393224 | tf_op jit(solution)/shard_map/ppermute | solution.py:24
  9.7 22.6 %collective-permute-start = (bf16[128,512]{1,0:T(8,128)(2,1)}, bf16[128,512]{1,0:T(8,128)(2,1)S(1)}, u32[]{:S(2)}, u32[]{:S(2)}) collective-permute-start(bf16[128,512]{1,0:T(8,128)(2,1)} %constant_dynamic-update-slice_fusion), channel_id=1, source_target_pairs={{0,8},{2,10},{4,12},{6,14},{8,16},{10,18},{12,20},{14,22},{16,24},... | collective-permute-start | bytes 393224 | tf_op jit(solution)/shard_map/ppermute | solution.py:24
  13.2 94.3 %collective-permute-start.15 = (bf16[2048,256]{1,0:T(8,128)(2,1)}, bf16[2048,256]{1,0:T(8,128)(2,1)S(1)}, u32[]{:S(2)}, u32[]{:S(2)}) collective-permute-start(bf16[2048,256]{1,0:T(8,128)(2,1)} %refs_8_.3), channel_id=1, source_target_pairs={{0,2},{2,0},{4,6},{6,4},{8,10},{10,8},{12,14},{14,12},{16,18},{18,... | collective-permute-start | bytes 3145736 | tf_op jit(solution)/shard_map/ppermute | solution.py:18
  14.8 65.0 %collective-permute-start.12 = (bf16[512,128]{1,0:T(8,128)(2,1)}, bf16[512,128]{1,0:T(8,128)(2,1)}, u32[]{:S(2)}, u32[]{:S(2)}) collective-permute-start(bf16[512,128]{1,0:T(8,128)(2,1)} %slice.216), channel_id=1, source_target_pairs={{0,16},{2,18},{4,20},{6,22},{8,24},{10,26},{12,28},{14,30},{16,0},... | collective-permute-start | bytes 393224 | tf_op jit(solution)/shard_map/ppermute | solution.py:18
  29.3 51.4 %collective-permute-start.11 = (bf16[1536,128]{1,0:T(8,128)(2,1)}, bf16[1536,128]{1,0:T(8,128)(2,1)}, u32[]{:S(2)}, u32[]{:S(2)}) collective-permute-start(bf16[1536,128]{1,0:T(8,128)(2,1)} %slice.215), channel_id=1, source_target_pairs={{0,16},{2,18},{4,20},{6,22},{8,24},{10,26},{12,28},{14,30},{16,0},... | collective-permute-start | bytes 1179656 | tf_op jit(solution)/shard_map/ppermute | solution.py:18
  32.3 8.2 %collective-permute-start.2 = (bf16[2,128,512]{2,1,0:T(8,128)(2,1)S(1)}, bf16[2,128,512]{2,1,0:T(8,128)(2,1)S(1)}, u32[]{:S(2)}, u32[]{:S(2)}) collective-permute-start(bf16[2,128,512]{2,1,0:T(8,128)(2,1)S(1)} %pad_maximum_fusion), channel_id=1, source_target_pairs={{0,4},{2,6},{4,0},{6,2},{8,12},{10,14},{12,8},{14,10},{16,20},{18,... | collective-permute-start | bytes 786440 | tf_op jit(solution)/shard_map/ppermute | solution.py:18
  32.9 39.5 %collective-permute-start.20 = (bf16[2048,128]{1,0:T(8,128)(2,1)}, bf16[2048,128]{1,0:T(8,128)(2,1)}, u32[]{:S(2)}, u32[]{:S(2)}) collective-permute-start(bf16[2048,128]{1,0:T(8,128)(2,1)} %slice.229), channel_id=1, source_target_pairs={{0,16},{2,18},{4,20},{6,22},{8,24},{10,26},{12,28},{14,30},{16,0},... | collective-permute-start | bytes 1572872 | tf_op jit(solution)/shard_map/ppermute | solution.py:18
  40.5 31.9 %collective-permute-start.4 = (bf16[6,128,512]{2,1,0:T(8,128)(2,1)S(1)}, bf16[6,128,512]{2,1,0:T(8,128)(2,1)}, u32[]{:S(2)}, u32[]{:S(2)}) collective-permute-start(bf16[6,128,512]{2,1,0:T(8,128)(2,1)S(1)} %constant_dynamic-update-slice_fusion.2.a_ref), channel_id=1, source_target_pairs={{0,2},{2,0},{4,6},{6,4},{8,10},{10,8},{12,14},{14,12},{16,18},{18,... | collective-permute-start | bytes 2359304 | tf_op jit(solution)/shard_map/ppermute | solution.py:18
  72.4 20.8 %collective-permute-start.21 = (bf16[2048,128]{1,0:T(8,128)(2,1)}, bf16[2048,128]{1,0:T(8,128)(2,1)}, u32[]{:S(2)}, u32[]{:S(2)}) collective-permute-start(bf16[2048,128]{1,0:T(8,128)(2,1)} %collective-permute-done.20.refs_8_), channel_id=1, source_target_pairs={{0,2},{2,0},{4,6},{6,4},{8,10},{10,8},{12,14},{14,12},{16,18},{18,... | collective-permute-start | bytes 1572872 | tf_op jit(solution)/shard_map/ppermute | solution.py:18
  75.1 9.0 %collective-permute-start.7 = (bf16[128,1024]{1,0:T(8,128)(2,1)S(1)}, bf16[128,1024]{1,0:T(8,128)(2,1)S(1)}, u32[]{:S(2)}, u32[]{:S(2)}) collective-permute-start(bf16[128,1024]{1,0:T(8,128)(2,1)S(1)} %attend.2.refs_0_), channel_id=1, source_target_pairs={{0,8},{2,10},{4,12},{6,14},{8,0},{10,2},{12,4},{14,6},{16,24},{18,... | collective-permute-start | bytes 786440 | tf_op jit(solution)/shard_map/ppermute | solution.py:18
  79.8 9.2 %collective-permute-start.5 = (bf16[128,1024]{1,0:T(8,128)(2,1)S(1)}, bf16[128,1024]{1,0:T(8,128)(2,1)S(1)}, u32[]{:S(2)}, u32[]{:S(2)}) collective-permute-start(bf16[128,1024]{1,0:T(8,128)(2,1)S(1)} %attend.2.refs_0_), channel_id=1, source_target_pairs={{0,4},{2,6},{4,0},{6,2},{8,12},{10,14},{12,8},{14,10},{16,20},{18,... | collective-permute-start | bytes 786440 | tf_op jit(solution)/shard_map/ppermute | solution.py:18
  80.7 9.2 %collective-permute-start.8 = (bf16[128,1024]{1,0:T(8,128)(2,1)S(1)}, bf16[128,1024]{1,0:T(8,128)(2,1)S(1)}, u32[]{:S(2)}, u32[]{:S(2)}) collective-permute-start(bf16[128,1024]{1,0:T(8,128)(2,1)S(1)} %attend.3.refs_1_), channel_id=1, source_target_pairs={{0,8},{2,10},{4,12},{6,14},{8,0},{10,2},{12,4},{14,6},{16,24},{18,... | collective-permute-start | bytes 786440 | tf_op jit(solution)/shard_map/ppermute | solution.py:18
  84.1 10.7 %collective-permute-start.6 = (bf16[128,1024]{1,0:T(8,128)(2,1)S(1)}, bf16[128,1024]{1,0:T(8,128)(2,1)}, u32[]{:S(2)}, u32[]{:S(2)}) collective-permute-start(bf16[128,1024]{1,0:T(8,128)(2,1)S(1)} %attend.3.refs_1_), channel_id=1, source_target_pairs={{0,4},{2,6},{4,0},{6,2},{8,12},{10,14},{12,8},{14,10},{16,20},{18,... | collective-permute-start | bytes 786440 | tf_op jit(solution)/shard_map/ppermute | solution.py:18
  89.1 11.3 %collective-permute-start.9 = (bf16[128,1024]{1,0:T(8,128)(2,1)S(1)}, bf16[128,1024]{1,0:T(8,128)(2,1)}, u32[]{:S(2)}, u32[]{:S(2)}) collective-permute-start(bf16[128,1024]{1,0:T(8,128)(2,1)S(1)} %collective-permute-done.7.refs_4_), channel_id=1, source_target_pairs={{0,4},{2,6},{4,0},{6,2},{8,12},{10,14},{12,8},{14,10},{16,20},{18,... | collective-permute-start | bytes 786440 | tf_op jit(solution)/shard_map/ppermute | solution.py:18
  89.9 15.4 %collective-permute-start.10 = (bf16[128,1024]{1,0:T(8,128)(2,1)S(1)}, bf16[128,1024]{1,0:T(8,128)(2,1)}, u32[]{:S(2)}, u32[]{:S(2)}) collective-permute-start(bf16[128,1024]{1,0:T(8,128)(2,1)S(1)} %collective-permute-done.8.refs_5_), channel_id=1, source_target_pairs={{0,4},{2,6},{4,0},{6,2},{8,12},{10,14},{12,8},{14,10},{16,20},{18,... | collective-permute-start | bytes 786440 | tf_op jit(solution)/shard_map/ppermute | solution.py:18
  93.2 19.5 %collective-permute-start.14 = (bf16[512,128]{1,0:T(8,128)(2,1)}, bf16[512,128]{1,0:T(8,128)(2,1)S(1)}, u32[]{:S(2)}, u32[]{:S(2)}) collective-permute-start(bf16[512,128]{1,0:T(8,128)(2,1)} %collective-permute-done.12.refs_9_), channel_id=1, source_target_pairs={{0,2},{2,0},{4,6},{6,4},{8,10},{10,8},{12,14},{14,12},{16,18},{18,... | collective-permute-start | bytes 393224 | tf_op jit(solution)/shard_map/ppermute | solution.py:18
  94.8 17.9 %collective-permute-start.13 = (bf16[1536,128]{1,0:T(8,128)(2,1)}, bf16[1536,128]{1,0:T(8,128)(2,1)S(1)}, u32[]{:S(2)}, u32[]{:S(2)}) collective-permute-start(bf16[1536,128]{1,0:T(8,128)(2,1)} %collective-permute-done.11.refs_8_), channel_id=1, source_target_pairs={{0,2},{2,0},{4,6},{6,4},{8,10},{10,8},{12,14},{14,12},{16,18},{18,... | collective-permute-start | bytes 1179656 | tf_op jit(solution)/shard_map/ppermute | solution.py:18
  109.3 8.1 %collective-permute-start.22 = (bf16[512,256]{1,0:T(8,128)(2,1)S(1)}, bf16[512,256]{1,0:T(8,128)(2,1)S(1)}, u32[]{:S(2)}, u32[]{:S(2)}) collective-permute-start(bf16[512,256]{1,0:T(8,128)(2,1)S(1)} %broadcast_select_fusion), channel_id=1, source_target_pairs={{0,1},{1,0},{2,3},{3,2},{4,5},{5,4},{6,7},{7,6},{8,9},{9,8},{10,11... | collective-permute-start | bytes 786440 | tf_op jit(solution)/shard_map/ppermute | solution.py:18
  114.8 7.8 %collective-permute-start.16 = (bf16[512,256]{1,0:T(8,128)(2,1)S(1)}, bf16[512,256]{1,0:T(8,128)(2,1)S(1)}, u32[]{:S(2)}, u32[]{:S(2)}) collective-permute-start(bf16[512,256]{1,0:T(8,128)(2,1)S(1)} %broadcast_select_fusion.1), channel_id=1, source_target_pairs={{0,1},{1,0},{2,3},{3,2},{4,5},{5,4},{6,7},{7,6},{8,9},{9,8},{10,11... | collective-permute-start | bytes 786440 | tf_op jit(solution)/shard_map/ppermute | solution.py:18
  117.6 9.1 %collective-permute-start.24 = (bf16[128,256]{1,0:T(8,128)(2,1)S(1)}, bf16[128,256]{1,0:T(8,128)(2,1)S(1)}, u32[]{:S(2)}, u32[]{:S(2)}) collective-permute-start(bf16[128,256]{1,0:T(8,128)(2,1)S(1)} %get-tuple-element.49), channel_id=1, source_target_pairs={{0,8},{2,10},{4,12},{6,14},{8,0},{10,2},{12,4},{14,6},{16,24},{18,... | collective-permute-start | bytes 196616 | tf_op jit(solution)/shard_map/ppermute | solution.py:18
  119.8 6.8 %collective-permute-start.25 = (bf16[128,256]{1,0:T(8,128)(2,1)S(1)}, bf16[128,256]{1,0:T(8,128)(2,1)S(1)}, u32[]{:S(2)}, u32[]{:S(2)}) collective-permute-start(bf16[128,256]{1,0:T(8,128)(2,1)S(1)} %get-tuple-element.50), channel_id=1, source_target_pairs={{0,12},{2,14},{4,8},{6,10},{8,4},{10,6},{12,0},{14,2},{16,28},{18,... | collective-permute-start | bytes 196616 | tf_op jit(solution)/shard_map/ppermute | solution.py:18
  120.3 5.3 %collective-permute-start.23 = (bf16[128,256]{1,0:T(8,128)(2,1)S(1)}, bf16[128,256]{1,0:T(8,128)(2,1)S(1)}, u32[]{:S(2)}, u32[]{:S(2)}) collective-permute-start(bf16[128,256]{1,0:T(8,128)(2,1)S(1)} %get-tuple-element.51), channel_id=1, source_target_pairs={{0,4},{2,6},{4,0},{6,2},{8,12},{10,14},{12,8},{14,10},{16,20},{18,... | collective-permute-start | bytes 196616 | tf_op jit(solution)/shard_map/ppermute | solution.py:18
  122.7 7.6 %collective-permute-start.18 = (bf16[128,256]{1,0:T(8,128)(2,1)S(1)}, bf16[128,256]{1,0:T(8,128)(2,1)S(1)}, u32[]{:S(2)}, u32[]{:S(2)}) collective-permute-start(bf16[128,256]{1,0:T(8,128)(2,1)S(1)} %get-tuple-element.52), channel_id=1, source_target_pairs={{0,8},{2,10},{4,12},{6,14},{8,0},{10,2},{12,4},{14,6},{16,24},{18,... | collective-permute-start | bytes 196616 | tf_op jit(solution)/shard_map/ppermute | solution.py:18
  (15 other events, 162.9 us)
